TPU v7x, 32 devices: a whole 2x2x4 slice. The times are simulated.
32 devices in a mesh: rep: 2 (over x), zero: 16 (over z, y, core).
Axes of the slice: x: 2, y: 2, z: 4, core: 2. Of those that a mesh axis runs over, the one named last changes fastest.
Arguments:
- acts: bfloat16 [256, 8192], P('rep', 'zero'), may hold values from -6 to 6
- grads_out: bfloat16 [256, 8192], P('rep', 'zero'), may hold values from -12 to 12
- act_inverse: bfloat16 [8192, 8192], P('zero'), as said below
- grad_inverse: bfloat16 [8192, 8192], P('zero'), as said below
Outputs:
- precond: float32 [8192, 8192], P('zero')
Inputs may be any that keep to these rules, and one draw needn't show every extreme that they name: act_inverse is symmetric. grad_inverse is symmetric.
All inputs are finite; a program needn't handle non-finite values.
Results may differ from a plain program's by a relative error of at most 0.004.
Values may be sent and summed in bfloat16 or wider, within the bound.
A program may use at most 128 MiB of HBM per device.

v0:
```python
import functools

import jax
import jax.numpy as jnp
from jax import lax
from jax.experimental import pallas as pl
from jax.experimental.pallas import tpu as pltpu
from jax.sharding import PartitionSpec as P

NT = (((1,), (1,)), ((), ()))


def gathered(acts, grads_out, act_inverse, grad_inverse):
    group = acts.shape[0]
    total_tokens = group * lax.axis_size("rep")
    both = lax.all_gather(jnp.concatenate([acts, grads_out], 0), "zero", axis=1, tiled=True)
    act_own = lax.dot_general(
        both[:group], act_inverse, NT, preferred_element_type=jnp.float32
    ).astype(jnp.bfloat16)
    act_pre = lax.all_gather(act_own, ("rep", "zero"), axis=0)
    grad_own = lax.dot_general(
        both[group:], grad_inverse, NT, preferred_element_type=jnp.float32
    ).astype(jnp.bfloat16)
    grad_pre = lax.all_gather(grad_own, "rep", axis=0, tiled=True)
    zero = lax.axis_size("zero")
    act_pre = act_pre.reshape(-1, zero, group, act_own.shape[1]).transpose(0, 2, 1, 3)
    act_pre = act_pre.reshape(total_tokens, -1)
    summed = lax.dot_general(
        grad_pre, act_pre, (((0,), (0,)), ((), ())), preferred_element_type=jnp.float32
    )
    return summed / jnp.float32(total_tokens)


MESH = pl.DeviceIdType.MESH


def gather_kernel(
    outer, acts, grads, a_hbm, g_hbm, pre, grad_pre,
    a_rows, g_rows, held, acc_a, acc_g,
    w_sem, send1, recv1, send2, recv2, x_send, x_recv, own_sem,
):
    width = acts.shape[1]
    zero = outer * 4
    rep = lax.axis_index("rep")
    me = lax.axis_index("zero")
    z, y, c = me // 4, (me // 2) % 2, me % 2
    other_y, other_c, other_rep = 1 - y, 1 - c, 1 - rep

    def at(dz, yy, cc):
        return ((z + dz) % outer) * 4 + yy * 2 + cc

    own = [
        pltpu.make_async_copy(acts, held.at[0, me], own_sem.at[0]),
        pltpu.make_async_copy(grads, held.at[1, me], own_sem.at[1]),
    ]
    for load in own:
        load.start()
    loads = [
        pltpu.make_async_copy(a_hbm, a_rows, w_sem.at[0]),
        pltpu.make_async_copy(g_hbm, g_rows, w_sem.at[1]),
    ]
    for load in loads:
        load.start()

    hops = list(range(1, outer))
    hops.sort(key=lambda d: min(d, outer - d))
    peers = [(rep, at(d, y, c)) for d in hops]
    peers += [(rep, at(0, other_y, c)), (rep, at(0, y, other_c)), (other_rep, me)]
    barrier = pltpu.get_barrier_semaphore()
    for peer in peers:
        pl.semaphore_signal(barrier, inc=1, device_id=peer, device_id_type=MESH)
    pl.semaphore_wait(barrier, len(peers))

    sent = []

    def send1_to(q, slot, block, source, peer):
        copy = pltpu.make_async_remote_copy(
            src_ref=source, dst_ref=held.at[q, block],
            send_sem=send1.at[q, slot], recv_sem=recv1.at[q, block],
            device_id=peer, device_id_type=MESH,
        )
        copy.start()
        sent.append(copy)

    def wait1(q, block):
        pltpu.make_async_copy(held.at[q, block], held.at[q, block], recv1.at[q, block]).wait()

    z_peer = {d: (rep, at(d, y, c)) for d in hops}
    y_peer = (rep, at(0, other_y, c))
    c_peer = (rep, at(0, y, other_c))
    y_slot, c_slot = outer, 2 * outer

    for q in range(2):
        own[q].wait()
        for d in hops:
            send1_to(q, d, me, held.at[q, me], z_peer[d])
        send1_to(q, y_slot, me, held.at[q, me], y_peer)
        send1_to(q, c_slot, me, held.at[q, me], c_peer)

    def columns(block):
        return pl.ds(pl.multiple_of(block * width, width), width)

    def add(q, block, value):
        if q == 0:
            acc_a[...] += lax.dot_general(
                value, a_rows[:, columns(block)], NT, preferred_element_type=jnp.float32
            )
        else:
            acc_g[...] += lax.dot_general(
                g_rows[:, columns(block)], value, NT, preferred_element_type=jnp.float32
            )

    def from_z(q, ds):
        for d in ds:
            block = at(d, y, c)
            wait1(q, block)
            send1_to(q, y_slot + d, block, held.at[q, block], y_peer)
            send1_to(q, c_slot + d, block, held.at[q, block], c_peer)
            add(q, block, held[q, block])

    def from_y(q):
        for d in [0] + hops:
            block = at(d, other_y, c)
            wait1(q, block)
            send1_to(q, c_slot + outer + d, block, held.at[q, block], c_peer)
            add(q, block, held[q, block])

    def add_partner(q):
        for yy in (y, other_y):
            for d in [0] + hops:
                block = at(d, yy, other_c)
                wait1(q, block)
                add(q, block, held[q, block])

    acc_a[...] = jnp.zeros_like(acc_a)
    acc_g[...] = jnp.zeros_like(acc_g)
    loads[0].wait()
    add(0, me, held[0, me])
    from_z(0, hops)
    from_y(0)
    loads[1].wait()
    from_z(1, hops[:-1])
    add_partner(0)

    rep1, y1 = (rep + c) % 2, (y + 1 - c) % 2
    rep2, y2 = (rep + 1 - c) % 2, (y + c) % 2
    rep3, y3 = (rep2 + c) % 2, (y2 + 1 - c) % 2

    def send2_to(slot, block, peer):
        copy = pltpu.make_async_remote_copy(
            src_ref=pre.at[block], dst_ref=pre.at[block],
            send_sem=send2.at[slot], recv_sem=recv2.at[block],
            device_id=peer, device_id_type=MESH,
        )
        copy.start()
        sent.append(copy)

    def wait2(block):
        pltpu.make_async_copy(pre.at[block], pre.at[block], recv2.at[block]).wait()

    first_peer = (rep1, at(0, y1, c))
    second_peer = (rep2, at(0, y2, c))
    s1, s2, s3 = outer, 2 * outer, 4 * outer
    mine = rep * zero + me
    pre[mine] = acc_a[...].astype(jnp.bfloat16)

    from_z(1, hops[-1:])
    for d in hops:
        send2_to(d, mine, z_peer[d])
    send2_to(s1, mine, first_peer)
    send2_to(s2, mine, second_peer)
    send2_to(s3, mine, c_peer)

    add(1, me, held[1, me])
    from_y(1)
    for d in hops:
        block = rep * zero + at(d, y, c)
        wait2(block)
        send2_to(s1 + d, block, first_peer)
        send2_to(s2 + d, block, second_peer)
        send2_to(s3 + d, block, c_peer)
    add_partner(1)
    grad_pre[rep] = acc_g[...].astype(jnp.bfloat16)
    for i, d in enumerate([0] + hops):
        block = rep1 * zero + at(d, y1, c)
        wait2(block)
        send2_to(s2 + outer + d, block, second_peer)
        send2_to(s3 + outer + d, block, c_peer)
        if i == 0:
            swap = pltpu.make_async_remote_copy(
                src_ref=grad_pre.at[rep], dst_ref=grad_pre.at[rep],
                send_sem=x_send, recv_sem=x_recv,
                device_id=(other_rep, me), device_id_type=MESH,
            )
            swap.start()
    for part, (rr, yy) in enumerate(((rep2, y2), (rep3, y3))):
        for d in [0] + hops:
            block = rr * zero + at(d, yy, c)
            wait2(block)
            send2_to(s3 + (2 + part) * outer + d, block, c_peer)
    swap.wait()
    for rr in (rep, other_rep):
        for yy in (y, other_y):
            for d in [0] + hops:
                wait2(rr * zero + at(d, yy, other_c))
    for copy in sent:
        copy.wait_send()


SLOTS = 4


def product_kernel(grad_ref, act_ref, out_hbm, tiles, sems):
    reps, zero, group, width = act_ref.shape
    tokens = reps * group
    rows = jnp.concatenate([grad_ref[r] for r in range(reps)], axis=1)
    copies = []
    for i in range(zero):
        slot = i % SLOTS
        if i >= SLOTS:
            copies[i - SLOTS].wait()
        block = jnp.concatenate([act_ref[r, i] for r in range(reps)], axis=0)
        summed = jnp.dot(rows, block, preferred_element_type=jnp.float32)
        if tokens & (tokens - 1):
            tiles[slot] = summed / jnp.float32(tokens)
        else:
            tiles[slot] = summed * jnp.float32(1 / tokens)
        copy = pltpu.make_async_copy(
            tiles.at[slot], out_hbm.at[:, pl.ds(i * width, width)], sems.at[slot]
        )
        copy.start()
        copies.append(copy)
    for copy in copies[-SLOTS:]:
        copy.wait()


def fused(acts, grads_out, act_inverse, grad_inverse):
    group, width = acts.shape
    zero = lax.axis_size("zero")
    reps = lax.axis_size("rep")
    rows, cols = act_inverse.shape
    outer = zero // 4
    bf16, dma = jnp.bfloat16, pltpu.SemaphoreType.DMA
    vmem = pl.BlockSpec(memory_space=pltpu.VMEM)
    hbm = pl.BlockSpec(memory_space=pltpu.HBM)
    act_pre, grad_pre = pl.pallas_call(
        functools.partial(gather_kernel, outer),
        out_shape=(
            jax.ShapeDtypeStruct((reps * zero, group, width), bf16),
            jax.ShapeDtypeStruct((reps, width, group), bf16),
        ),
        in_specs=[hbm, hbm, hbm, hbm],
        out_specs=(vmem, vmem),
        scratch_shapes=[
            pltpu.VMEM((rows, cols), bf16),
            pltpu.VMEM((rows, cols), bf16),
            pltpu.VMEM((2, zero, group, width), bf16),
            pltpu.VMEM((group, width), jnp.float32),
            pltpu.VMEM((width, group), jnp.float32),
            dma((2,)),
            dma((2, 4 * outer)),
            dma((2, zero)),
            dma((8 * outer,)),
            dma((reps * zero,)),
            dma,
            dma,
            dma((2,)),
        ],
        compiler_params=pltpu.CompilerParams(
            collective_id=0, has_side_effects=True, vmem_limit_bytes=59 * 1024 * 1024
        ),
    )(acts, grads_out, act_inverse, grad_inverse)
    return pl.pallas_call(
        product_kernel,
        out_shape=jax.ShapeDtypeStruct((rows, cols), jnp.float32),
        in_specs=[vmem, vmem],
        out_specs=hbm,
        scratch_shapes=[pltpu.VMEM((SLOTS, rows, width), jnp.float32), dma((SLOTS,))],
        compiler_params=pltpu.CompilerParams(vmem_limit_bytes=32 * 1024 * 1024),
    )(grad_pre, act_pre.reshape(reps, zero, group, width))


def on_device(acts, grads_out, act_inverse, grad_inverse):
    whole = acts.shape[1] % 128 == 0 and acts.shape[0] % 128 == 0
    if whole and lax.axis_size("rep") == 2 and lax.axis_size("zero") % 4 == 0 and lax.axis_size("zero") > 4:
        return fused(acts, grads_out, act_inverse, grad_inverse)
    return gathered(acts, grads_out, act_inverse, grad_inverse)


def solution(mesh):
    return jax.shard_map(
        on_device,
        mesh=mesh,
        in_specs=(P("rep", "zero"), P("rep", "zero"), P("zero", None), P("zero", None)),
        out_specs=P("zero", None),
        check_vma=False,
    )
```

profile of v0, /device:TPU:0, one launch (start us, length us, event | category | flops | bytes accessed | tf_op | source)
XLA Modules:
  0.0 71.4 jit_solution(5071917825218478518)
XLA Ops:
  0.0 62.1 %shard_map.46 = (bf16[32,128,512]{2,1,0:T(8,128)(2,1)}, bf16[2,512,128]{2,1,0:T(8,128)(2,1)}) custom-call(bf16[128,512]{1,0:T(8,128)(2,1)} %acts.1, bf16[128,512]{1,0:T(8,128)(2,1)} %grads.1, bf16[512,8192]{1,0:T(8,128)(2,1)} %a_hbm.1, bf16[512,8192]{1,0:T(8,128)(2,1)} %g_hbm.1), custom_call_target="tpu_custom_call" | custom-call | tf_op jit(solution)/shard_map/pallas_call | solution.py:246
  62.1 0.0 copy-start
  62.1 2.2 %copy-done = bf16[32,128,512]{2,1,0:T(8,128)(2,1)S(1)} copy-done((bf16[32,128,512]{2,1,0:T(8,128)(2,1)S(1)}, bf16[32,128,512]{2,1,0:T(8,128)(2,1)}, u32[]{:S(2)}) %copy-start) | copy-done | bytes 4194328
  64.3 0.0 copy-start.1
  64.3 0.9 %copy-done.1 = bf16[2,512,128]{2,1,0:T(8,128)(2,1)S(1)} copy-done((bf16[2,512,128]{2,1,0:T(8,128)(2,1)S(1)}, bf16[2,512,128]{2,1,0:T(8,128)(2,1)}, u32[]{:S(2)}) %copy-start.1) | copy-done | bytes 262168
  65.3 6.2 %shard_map.47 = f32[512,8192]{1,0:T(8,128)} custom-call(bf16[2,512,128]{2,1,0:T(8,128)(2,1)S(1)} %copy-done.1, bf16[2,16,128,512]{3,2,1,0:T(8,128)(2,1)S(1)} %bitcast.1), custom_call_target="tpu_custom_call" | custom-call | tf_op jit(solution)/shard_map/pallas_call | solution.py:273
Async XLA Ops:
  62.1 2.2 %copy-start = (bf16[32,128,512]{2,1,0:T(8,128)(2,1)S(1)}, bf16[32,128,512]{2,1,0:T(8,128)(2,1)}, u32[]{:S(2)}) copy-start(bf16[32,128,512]{2,1,0:T(8,128)(2,1)} %get-tuple-element.8) | copy-start | bytes 12582916
  64.3 0.9 %copy-start.1 = (bf16[2,512,128]{2,1,0:T(8,128)(2,1)S(1)}, bf16[2,512,128]{2,1,0:T(8,128)(2,1)}, u32[]{:S(2)}) copy-start(bf16[2,512,128]{2,1,0:T(8,128)(2,1)} %get-tuple-element.7.grad_ref) | copy-start | bytes 786436
where the time goes:
time: 71.6 us; the launch traced here: 71.4 us
  Pallas kernels  68.3 us (95%)
  local copies, waits for them, and re-layouts  3.13 us (4%)
    pallas_call x1, Pallas kernels, fused(): pl.pallas_call(functools.partial(gather_kernel, outer), out_shape=(jax.Sh...  62.1 us
    pallas_call x1, Pallas kernels, fused(): pl.pallas_call(product_kernel, out_shape=jax.ShapeDtypeStruct((rows, cols...  6.17 us
    unnamed x4, local copies, waits for them, and re-layouts  3.13 us

commit v1 on v0

v1 whole, which is shorter than its diff:
```python
import functools

import jax
import jax.numpy as jnp
from jax import lax
from jax.experimental import pallas as pl
from jax.experimental.pallas import tpu as pltpu
from jax.sharding import PartitionSpec as P

NT = (((1,), (1,)), ((), ()))


def gathered(acts, grads_out, act_inverse, grad_inverse):
    group = acts.shape[0]
    total_tokens = group * lax.axis_size("rep")
    both = lax.all_gather(jnp.concatenate([acts, grads_out], 0), "zero", axis=1, tiled=True)
    act_own = lax.dot_general(
        both[:group], act_inverse, NT, preferred_element_type=jnp.float32
    ).astype(jnp.bfloat16)
    act_pre = lax.all_gather(act_own, ("rep", "zero"), axis=0)
    grad_own = lax.dot_general(
        both[group:], grad_inverse, NT, preferred_element_type=jnp.float32
    ).astype(jnp.bfloat16)
    grad_pre = lax.all_gather(grad_own, "rep", axis=0, tiled=True)
    zero = lax.axis_size("zero")
    act_pre = act_pre.reshape(-1, zero, group, act_own.shape[1]).transpose(0, 2, 1, 3)
    act_pre = act_pre.reshape(total_tokens, -1)
    summed = lax.dot_general(
        grad_pre, act_pre, (((0,), (0,)), ((), ())), preferred_element_type=jnp.float32
    )
    return summed / jnp.float32(total_tokens)


MESH = pl.DeviceIdType.MESH

PIECES = (4, 2, 2)
SWAPPED = (0, 0, 1)
ROUND_Y, ROUND_Z = 2, 1
KERNEL_VMEM = 46137344


ORDERS = {4: [('own', 0), ('near', 0, 0, 0, 0, 1), ('near', 0, 0, 0, 0, 2), ('near', 0, 1, 0, 0, 1), ('near', 0, 1, 0, 1, 0), ('near', 0, 1, 0, 0, 2), ('near', 0, 3, 0, 0, 1), ('near', 0, 3, 0, 0, 2), ('near', 0, 2, 0, 0, 1), ('near', 0, 0, 0, 1, 1), ('near', 0, 1, 0, 0, 3), ('near', 0, 0, 0, 1, 0), ('near', 0, 0, 0, 0, 3), ('near', 0, 2, 0, 0, 2), ('near', 0, 1, 0, 1, 1), ('near', 0, 2, 0, 1, 0), ('near', 0, 3, 0, 0, 3), ('near', 0, 3, 0, 1, 1), ('near', 0, 3, 0, 1, 0), ('near', 0, 2, 0, 0, 3), ('partner', 0, 0, 0, 2), ('own', 1), ('near', 0, 1, 0, 1, 2), ('near', 0, 2, 0, 1, 1), ('partner', 0, 0, 0, 1), ('near', 0, 3, 0, 1, 2), ('partner', 0, 0, 1, 1), ('near', 0, 0, 0, 1, 2), ('near', 0, 2, 0, 1, 2), ('partner', 0, 0, 0, 0), ('partner', 0, 0, 1, 0), ('near', 1, 0, 0, 0, 2), ('partner', 0, 0, 0, 3), ('near', 0, 3, 0, 1, 3), ('near', 0, 0, 0, 1, 3), ('near', 0, 1, 0, 1, 3), ('near', 0, 2, 0, 1, 3), ('partner', 1, 0, 0, 0), ('partner', 0, 0, 1, 2), ('near', 1, 1, 0, 0, 2), ('partner', 0, 0, 1, 3), ('own', 2), ('near', 2, 0, 0, 0, 2), ('near', 1, 0, 0, 0, 1), ('near', 2, 1, 0, 0, 2), ('near', 2, 1, 0, 1, 0), ('near', 1, 1, 0, 1, 0), ('near', 2, 0, 0, 0, 1), ('near', 1, 1, 0, 0, 1), ('near', 2, 0, 0, 1, 2), ('near', 2, 0, 0, 1, 0), ('near', 1, 1, 0, 1, 2), ('near', 2, 1, 0, 0, 1), ('near', 1, 0, 0, 0, 3), ('partner', 1, 0, 0, 2), ('near', 2, 1, 0, 1, 2), ('near', 2, 0, 0, 1, 1), ('near', 1, 0, 0, 1, 0), ('near', 2, 0, 1, 0, 0), ('near', 2, 1, 0, 1, 1), ('near', 1, 0, 0, 1, 2), ('partner', 1, 0, 1, 0), ('near', 1, 1, 0, 0, 3), ('near', 1, 0, 0, 1, 1), ('partner', 1, 0, 0, 1), ('near', 1, 1, 0, 1, 1), ('near', 2, 0, 0, 0, 3), ('near', 2, 1, 0, 0, 3), ('near', 2, 1, 1, 0, 1), ('partner', 1, 0, 1, 1), ('near', 2, 1, 1, 0, 0), ('near', 2, 0, 1, 0, 1), ('near', 2, 1, 0, 1, 3), ('near', 1, 1, 0, 1, 3), ('near', 1, 0, 0, 1, 3), ('near', 2, 0, 1, 1, 1), ('near', 2, 0, 1, 0, 3), ('near', 2, 0, 0, 1, 3), ('partner', 1, 0, 1, 2), ('partner', 1, 0, 1, 3), ('partner', 1, 0, 0, 3), ('near', 2, 0, 1, 1, 0), ('near', 2, 1, 1, 1, 2), ('near', 2, 0, 1, 0, 2), ('near', 2, 1, 1, 0, 2), ('near', 2, 1, 1, 1, 0), ('swap', 1), ('near', 2, 1, 1, 1, 3), ('near', 2, 0, 1, 1, 2), ('near', 2, 1, 1, 1, 1), ('near', 2, 1, 1, 0, 3), ('near', 2, 0, 1, 1, 3), ('partner', 2, 0, 0, 0), ('partner', 2, 0, 0, 1), ('partner', 2, 0, 0, 2), ('partner', 2, 0, 0, 3), ('partner', 2, 0, 1, 0), ('partner', 2, 0, 1, 1), ('partner', 2, 0, 1, 2), ('partner', 2, 0, 1, 3), ('partner', 2, 1, 0, 0), ('partner', 2, 1, 0, 1), ('partner', 2, 1, 0, 2), ('partner', 2, 1, 0, 3), ('partner', 2, 1, 1, 0), ('partner', 2, 1, 1, 1), ('partner', 2, 1, 1, 2), ('partner', 2, 1, 1, 3)]}


def schedule(outer):
    return ORDERS[outer]


def nearest_first(outer):
    rows = []
    for z in range(outer):
        others = [q for q in range(outer) if q != z]
        others.sort(key=lambda q: (abs(q - z), q if 2 * z < outer else -q))
        rows.append([z] + others)
    return rows


def hops(kind, unit, r, yy, j):
    by_y, by_z = unit < ROUND_Y, unit < ROUND_Z
    if r == 1:
        if yy == 0 and j == 0:
            return ["y"] * by_y + ["up", "down"] * by_z
        return []
    ways = []
    if kind == 2:
        if yy == 1 and j == 0:
            ways += ["x"] * (not by_y)
        elif yy == 0 and j in (1, 2) and by_z:
            ways += ["x far"] * (j == 2)
        else:
            ways += ["x"]
    late = unit >= PIECES[kind] - SWAPPED[kind]
    if yy == 0 or late:
        ways += ["up", "down"] if j == 0 else ["on"]
    if yy == 0 and (j == 0 or not late):
        ways += ["y"]
    return ways


def sends_of(order):
    count, seen = 0, {}
    for what, kind, *rest in order:
        if what == "own":
            count += 1 + sum(len(hops(kind, unit, 0, 0, 0)) for unit in range(PIECES[kind]))
        elif what == "near":
            key = (kind, *rest[1:])
            seen[key] = seen.get(key, 0) + 1
            count += len(hops(kind, *rest)) + (seen[key] == PIECES[kind])
    return count


def gather_kernel(
    outer, order, acts, grads, a_hbm, g_hbm, pre, grad_pre,
    a_rows, g_rows, held, acc_a, acc_g,
    w_sem, send_sem, recv, recv_pre, x_recv, own_sem,
):
    group, width = acts.shape
    zero = outer * 4
    rep = lax.axis_index("rep")
    me = lax.axis_index("zero")
    z, y, c = me // 4, (me // 2) % 2, me % 2

    own = [
        pltpu.make_async_copy(acts, held.at[0, me], own_sem.at[0]),
        pltpu.make_async_copy(grads, held.at[1, me], own_sem.at[1]),
    ]
    loads = [
        pltpu.make_async_copy(a_hbm, a_rows, w_sem.at[0]),
        pltpu.make_async_copy(g_hbm, g_rows, w_sem.at[1]),
    ]
    own[0].start()
    own[1].start()
    loads[0].start()

    x_peer = (1 - rep, me)
    y_peer = (rep, z * 4 + (1 - y) * 2 + c)
    c_peer = (rep, z * 4 + y * 2 + 1 - c)
    has_up, has_down = z < outer - 1, z > 0

    def z_peer(to):
        return (rep, to * 4 + y * 2 + c)

    barrier = pltpu.get_barrier_semaphore()

    def greet(peer):
        pl.semaphore_signal(barrier, inc=1, device_id=peer, device_id_type=MESH)

    for peer in (x_peer, y_peer, c_peer):
        greet(peer)
    pl.when(has_up)(lambda: greet(z_peer(z + 1)))
    pl.when(has_down)(lambda: greet(z_peer(z - 1)))
    pl.semaphore_wait(barrier, 3 + has_up.astype(jnp.int32) + has_down.astype(jnp.int32))

    table = nearest_first(outer)
    at_z = []
    for j in range(outer):
        value = jnp.int32(table[0][j])
        for q in range(1, outer):
            value = jnp.where(z == q, table[q][j], value)
        at_z.append(value)

    def block_of(kind, r, yy, j, other=False):
        cc = 1 - c if other else c
        block = at_z[j] * 4 + ((y + yy) % 2) * 2 + cc
        if kind == 2:
            block += ((rep + r) % 2) * zero
        return block

    def view(kind, block, unit=None):
        ref = pre.at[block] if kind == 2 else held.at[kind, block]
        if unit is None:
            return ref
        rows = group // PIECES[kind]
        return ref.at[pl.ds(unit * rows, rows)]

    def landing(kind, block, unit):
        return recv_pre.at[block, unit] if kind == 2 else recv.at[kind, block, unit]

    sent = []

    def send(ref, peer, arrival, when=None):
        copy = pltpu.make_async_remote_copy(
            src_ref=ref, dst_ref=ref,
            send_sem=send_sem.at[len(sent)], recv_sem=arrival,
            device_id=peer, device_id_type=MESH,
        )
        sent.append((copy, when))
        if when is None:
            copy.start()
        else:
            pl.when(when)(copy.start)

    def forward(kind, unit, r, yy, j):
        block = block_of(kind, r, yy, j)
        ref, arrival = view(kind, block, unit), landing(kind, block, unit)
        onward = jnp.where(at_z[j] < z, z + 1, z - 1)
        ways = {
            "x": (x_peer, None),
            "x far": (x_peer, jnp.abs(at_z[j] - z) > 1),
            "y": (y_peer, None),
            "up": (z_peer(z + 1), has_up),
            "down": (z_peer(z - 1), has_down),
            "on": (z_peer(onward), (onward >= 0) & (onward < outer)),
        }
        for way in hops(kind, unit, r, yy, j):
            peer, when = ways[way]
            send(ref, peer, arrival, when)

    def to_partner(kind, r, yy, j):
        block = block_of(kind, r, yy, j)
        send(view(kind, block), c_peer, landing(kind, block, 0))

    begun = [False, False]

    def add(kind, block):
        value = held[kind, block]
        columns = pl.ds(pl.multiple_of(block * width, width), width)
        if kind == 0:
            acc, term = acc_a, lax.dot_general(
                value, a_rows[:, columns], NT, preferred_element_type=jnp.float32
            )
        else:
            acc, term = acc_g, lax.dot_general(
                g_rows[:, columns], value, NT, preferred_element_type=jnp.float32
            )
        if begun[kind]:
            acc[...] += term
        else:
            acc[...] = term
            begun[kind] = True

    def wait(ref, arrival):
        pltpu.make_async_copy(ref, ref, arrival).wait()

    mine = rep * zero + me
    arrived = {}
    swap = pltpu.make_async_remote_copy(
        src_ref=grad_pre.at[rep], dst_ref=grad_pre.at[rep],
        send_sem=own_sem.at[2], recv_sem=x_recv,
        device_id=x_peer, device_id_type=MESH,
    )
    for step in order:
        what, kind = step[0], step[1]
        if what == "own":
            if kind == 2:
                pre[mine] = acc_a[...].astype(jnp.bfloat16)
            else:
                own[kind].wait()
            for unit in range(PIECES[kind]):
                forward(kind, unit, 0, 0, 0)
            to_partner(kind, 0, 0, 0)
            if kind < 2:
                loads[kind].wait()
                if kind == 0:
                    loads[1].start()
                add(kind, me)
        elif what == "near":
            _, _, unit, r, yy, j = step
            block = block_of(kind, r, yy, j)
            wait(view(kind, block, unit), landing(kind, block, unit))
            forward(kind, unit, r, yy, j)
            arrived[kind, r, yy, j] = arrived.get((kind, r, yy, j), 0) + 1
            if arrived[kind, r, yy, j] == PIECES[kind]:
                to_partner(kind, r, yy, j)
                if kind < 2:
                    add(kind, block)
        elif what == "partner":
            _, _, r, yy, j = step
            block = block_of(kind, r, yy, j, True)
            wait(view(kind, block), landing(kind, block, 0))
            if kind < 2:
                add(kind, block)
        else:
            grad_pre[rep] = acc_g[...].astype(jnp.bfloat16)
            swap.start()
    swap.wait()
    for copy, when in sent:
        if when is None:
            copy.wait_send()
        else:
            pl.when(when)(copy.wait_send)


SLOTS = 4


def product_kernel(grad_ref, act_ref, out_hbm, tiles, sems):
    reps, zero, group, width = act_ref.shape
    tokens = reps * group
    rows = jnp.concatenate([grad_ref[r] for r in range(reps)], axis=1)
    copies = []
    for i in range(zero):
        slot = i % SLOTS
        if i >= SLOTS:
            copies[i - SLOTS].wait()
        block = jnp.concatenate([act_ref[r, i] for r in range(reps)], axis=0)
        summed = jnp.dot(rows, block, preferred_element_type=jnp.float32)
        if tokens & (tokens - 1):
            tiles[slot] = summed / jnp.float32(tokens)
        else:
            tiles[slot] = summed * jnp.float32(1 / tokens)
        copy = pltpu.make_async_copy(
            tiles.at[slot], out_hbm.at[:, pl.ds(i * width, width)], sems.at[slot]
        )
        copy.start()
        copies.append(copy)
    for copy in copies[-SLOTS:]:
        copy.wait()


def fused(acts, grads_out, act_inverse, grad_inverse):
    group, width = acts.shape
    zero = lax.axis_size("zero")
    reps = lax.axis_size("rep")
    rows, cols = act_inverse.shape
    outer = zero // 4
    bf16, dma = jnp.bfloat16, pltpu.SemaphoreType.DMA
    vmem = pl.BlockSpec(memory_space=pltpu.VMEM)
    hbm = pl.BlockSpec(memory_space=pltpu.HBM)
    order = schedule(outer)
    act_pre, grad_pre = pl.pallas_call(
        functools.partial(gather_kernel, outer, order),
        out_shape=(
            jax.ShapeDtypeStruct((reps * zero, group, width), bf16),
            jax.ShapeDtypeStruct((reps, width, group), bf16),
        ),
        in_specs=[hbm, hbm, hbm, hbm],
        out_specs=(vmem, vmem),
        scratch_shapes=[
            pltpu.VMEM((rows, cols), bf16),
            pltpu.VMEM((rows, cols), bf16),
            pltpu.VMEM((2, zero, group, width), bf16),
            pltpu.VMEM((group, width), jnp.float32),
            pltpu.VMEM((width, group), jnp.float32),
            dma((2,)),
            dma((sends_of(order),)),
            dma((2, zero, max(PIECES[:2]))),
            dma((reps * zero, PIECES[2])),
            dma,
            dma((3,)),
        ],
        compiler_params=pltpu.CompilerParams(
            collective_id=0, has_side_effects=True, vmem_limit_bytes=KERNEL_VMEM
        ),
    )(acts, grads_out, act_inverse, grad_inverse)
    return pl.pallas_call(
        product_kernel,
        out_shape=jax.ShapeDtypeStruct((rows, cols), jnp.float32),
        in_specs=[vmem, vmem],
        out_specs=hbm,
        scratch_shapes=[pltpu.VMEM((SLOTS, rows, width), jnp.float32), dma((SLOTS,))],
        compiler_params=pltpu.CompilerParams(vmem_limit_bytes=32 * 1024 * 1024),
    )(grad_pre, act_pre.reshape(reps, zero, group, width))


def on_device(acts, grads_out, act_inverse, grad_inverse):
    whole = acts.shape[1] % 128 == 0 and acts.shape[0] % 128 == 0
    if whole and lax.axis_size("rep") == 2 and lax.axis_size("zero") // 4 in ORDERS and lax.axis_size("zero") % 4 == 0:
        return fused(acts, grads_out, act_inverse, grad_inverse)
    return gathered(acts, grads_out, act_inverse, grad_inverse)


def solution(mesh):
    return jax.shard_map(
        on_device,
        mesh=mesh,
        in_specs=(P("rep", "zero"), P("rep", "zero"), P("zero", None), P("zero", None)),
        out_specs=P("zero", None),
        check_vma=False,
    )
```

time: 71.6 us -> 60.1 us (0.84)
  Pallas kernels: 68.3 us -> 58.1 us
  local copies, waits for them, and re-layouts: 3.13 us -> 1.81 us
    pallas_call x1, Pallas kernels: 62.1 us -> 51.9 us  [fused(): pl.pallas_call(functools.partial(gather_kernel, outer, order), out_shape=...]
    unnamed x4, local copies, waits for them, and re-layouts: 3.13 us -> 1.81 us
where the time goes in v1:
time: 60.1 us; the launch traced here: 59.9 us
  Pallas kernels  58.1 us (97%)
  local copies, waits for them, and re-layouts  1.81 us (3%)
    pallas_call x1, Pallas kernels, fused(): pl.pallas_call(functools.partial(gather_kernel, outer, order), out_shape=...  51.9 us
    pallas_call x1, Pallas kernels, fused(): pl.pallas_call(product_kernel, out_shape=jax.ShapeDtypeStruct((rows, cols...  6.17 us
    unnamed x4, local copies, waits for them, and re-layouts  1.81 us

profile of v1, /device:TPU:0, one launch (start us, length us, event | category | flops | bytes accessed | tf_op | source)
XLA Modules:
  0.0 59.9 jit_solution(14709485564338422527)
XLA Ops:
  0.0 0.0 copy-start
  0.0 0.9 %copy-done = bf16[128,512]{1,0:T(8,128)(2,1)S(1)} copy-done((bf16[128,512]{1,0:T(8,128)(2,1)S(1)}, bf16[128,512]{1,0:T(8,128)(2,1)}, u32[]{:S(2)}) %copy-start) | copy-done | bytes 131096
  0.9 0.0 copy-start.1
  0.9 0.9 %copy-done.1 = bf16[128,512]{1,0:T(8,128)(2,1)S(1)} copy-done((bf16[128,512]{1,0:T(8,128)(2,1)S(1)}, bf16[128,512]{1,0:T(8,128)(2,1)}, u32[]{:S(2)}) %copy-start.1) | copy-done | bytes 131096
  1.8 51.9 %shard_map.46 = (bf16[32,128,512]{2,1,0:T(8,128)(2,1)S(1)}, bf16[2,512,128]{2,1,0:T(8,128)(2,1)S(1)}) custom-call(bf16[128,512]{1,0:T(8,128)(2,1)S(1)} %copy-done, bf16[128,512]{1,0:T(8,128)(2,1)S(1)} %copy-done.1, bf16[512,8192]{1,0:T(8,128)(2,1)} %a_hbm.1, bf16[512,8192]{1,0:T(8,128)(2,1)} %g_hbm.1), custom_call_target="tpu_custom_call" | custom-call | tf_op jit(solution)/shard_map/pallas_call | solution.py:301
  53.8 6.2 %shard_map.47 = f32[512,8192]{1,0:T(8,128)} custom-call(bf16[2,512,128]{2,1,0:T(8,128)(2,1)S(1)} %get-tuple-element.7.grad_ref, bf16[2,16,128,512]{3,2,1,0:T(8,128)(2,1)S(1)} %bitcast.1), custom_call_target="tpu_custom_call" | custom-call | tf_op jit(solution)/shard_map/pallas_call | solution.py:326
Async XLA Ops:
  0.0 0.9 %copy-start = (bf16[128,512]{1,0:T(8,128)(2,1)S(1)}, bf16[128,512]{1,0:T(8,128)(2,1)}, u32[]{:S(2)}) copy-start(bf16[128,512]{1,0:T(8,128)(2,1)} %acts.1) | copy-start | bytes 393220
  0.9 0.9 %copy-start.1 = (bf16[128,512]{1,0:T(8,128)(2,1)S(1)}, bf16[128,512]{1,0:T(8,128)(2,1)}, u32[]{:S(2)}) copy-start(bf16[128,512]{1,0:T(8,128)(2,1)} %grads.1) | copy-start | bytes 393220

commit v2 on v1

--- a/solution.py
+++ b/solution.py
@@ -36,10 +36,10 @@
 PIECES = (4, 2, 2)
 SWAPPED = (0, 0, 1)
 ROUND_Y, ROUND_Z = 2, 1
+HOLD = 8
 KERNEL_VMEM = 46137344
 
-
-ORDERS = {4: [('own', 0), ('near', 0, 0, 0, 0, 1), ('near', 0, 0, 0, 0, 2), ('near', 0, 1, 0, 0, 1), ('near', 0, 1, 0, 1, 0), ('near', 0, 1, 0, 0, 2), ('near', 0, 3, 0, 0, 1), ('near', 0, 3, 0, 0, 2), ('near', 0, 2, 0, 0, 1), ('near', 0, 0, 0, 1, 1), ('near', 0, 1, 0, 0, 3), ('near', 0, 0, 0, 1, 0), ('near', 0, 0, 0, 0, 3), ('near', 0, 2, 0, 0, 2), ('near', 0, 1, 0, 1, 1), ('near', 0, 2, 0, 1, 0), ('near', 0, 3, 0, 0, 3), ('near', 0, 3, 0, 1, 1), ('near', 0, 3, 0, 1, 0), ('near', 0, 2, 0, 0, 3), ('partner', 0, 0, 0, 2), ('own', 1), ('near', 0, 1, 0, 1, 2), ('near', 0, 2, 0, 1, 1), ('partner', 0, 0, 0, 1), ('near', 0, 3, 0, 1, 2), ('partner', 0, 0, 1, 1), ('near', 0, 0, 0, 1, 2), ('near', 0, 2, 0, 1, 2), ('partner', 0, 0, 0, 0), ('partner', 0, 0, 1, 0), ('near', 1, 0, 0, 0, 2), ('partner', 0, 0, 0, 3), ('near', 0, 3, 0, 1, 3), ('near', 0, 0, 0, 1, 3), ('near', 0, 1, 0, 1, 3), ('near', 0, 2, 0, 1, 3), ('partner', 1, 0, 0, 0), ('partner', 0, 0, 1, 2), ('near', 1, 1, 0, 0, 2), ('partner', 0, 0, 1, 3), ('own', 2), ('near', 2, 0, 0, 0, 2), ('near', 1, 0, 0, 0, 1), ('near', 2, 1, 0, 0, 2), ('near', 2, 1, 0, 1, 0), ('near', 1, 1, 0, 1, 0), ('near', 2, 0, 0, 0, 1), ('near', 1, 1, 0, 0, 1), ('near', 2, 0, 0, 1, 2), ('near', 2, 0, 0, 1, 0), ('near', 1, 1, 0, 1, 2), ('near', 2, 1, 0, 0, 1), ('near', 1, 0, 0, 0, 3), ('partner', 1, 0, 0, 2), ('near', 2, 1, 0, 1, 2), ('near', 2, 0, 0, 1, 1), ('near', 1, 0, 0, 1, 0), ('near', 2, 0, 1, 0, 0), ('near', 2, 1, 0, 1, 1), ('near', 1, 0, 0, 1, 2), ('partner', 1, 0, 1, 0), ('near', 1, 1, 0, 0, 3), ('near', 1, 0, 0, 1, 1), ('partner', 1, 0, 0, 1), ('near', 1, 1, 0, 1, 1), ('near', 2, 0, 0, 0, 3), ('near', 2, 1, 0, 0, 3), ('near', 2, 1, 1, 0, 1), ('partner', 1, 0, 1, 1), ('near', 2, 1, 1, 0, 0), ('near', 2, 0, 1, 0, 1), ('near', 2, 1, 0, 1, 3), ('near', 1, 1, 0, 1, 3), ('near', 1, 0, 0, 1, 3), ('near', 2, 0, 1, 1, 1), ('near', 2, 0, 1, 0, 3), ('near', 2, 0, 0, 1, 3), ('partner', 1, 0, 1, 2), ('partner', 1, 0, 1, 3), ('partner', 1, 0, 0, 3), ('near', 2, 0, 1, 1, 0), ('near', 2, 1, 1, 1, 2), ('near', 2, 0, 1, 0, 2), ('near', 2, 1, 1, 0, 2), ('near', 2, 1, 1, 1, 0), ('swap', 1), ('near', 2, 1, 1, 1, 3), ('near', 2, 0, 1, 1, 2), ('near', 2, 1, 1, 1, 1), ('near', 2, 1, 1, 0, 3), ('near', 2, 0, 1, 1, 3), ('partner', 2, 0, 0, 0), ('partner', 2, 0, 0, 1), ('partner', 2, 0, 0, 2), ('partner', 2, 0, 0, 3), ('partner', 2, 0, 1, 0), ('partner', 2, 0, 1, 1), ('partner', 2, 0, 1, 2), ('partner', 2, 0, 1, 3), ('partner', 2, 1, 0, 0), ('partner', 2, 1, 0, 1), ('partner', 2, 1, 0, 2), ('partner', 2, 1, 0, 3), ('partner', 2, 1, 1, 0), ('partner', 2, 1, 1, 1), ('partner', 2, 1, 1, 2), ('partner', 2, 1, 1, 3)]}
+ORDERS = {4: [('own', 0), ('near', 0, 0, 0, 0, 1), ('near', 0, 0, 0, 0, 2), ('near', 0, 0, 0, 1, 0), ('near', 0, 1, 0, 0, 2), ('near', 0, 1, 0, 1, 0), ('near', 0, 3, 0, 0, 1), ('near', 0, 1, 0, 0, 1), ('near', 0, 0, 0, 1, 1), ('near', 0, 3, 0, 1, 0), ('near', 0, 2, 0, 0, 2), ('near', 0, 3, 0, 0, 2), ('near', 0, 2, 0, 0, 1), ('partner', 0, 0, 0, 0), ('near', 0, 0, 0, 0, 3), ('near', 0, 1, 0, 0, 3), ('near', 0, 2, 0, 0, 3), ('near', 0, 3, 0, 0, 3), ('near', 0, 1, 0, 1, 2), ('near', 0, 1, 0, 1, 1), ('near', 0, 2, 0, 1, 0), ('near', 0, 3, 0, 1, 2), ('partner', 0, 0, 0, 2), ('near', 0, 3, 0, 1, 1), ('near', 0, 2, 0, 1, 2), ('near', 0, 0, 0, 1, 2), ('own', 1), ('near', 0, 2, 0, 1, 1), ('partner', 0, 0, 0, 1), ('partner', 0, 0, 0, 3), ('partner', 0, 0, 1, 2), ('near', 0, 1, 0, 1, 3), ('partner', 0, 0, 1, 1), ('near', 0, 2, 0, 1, 3), ('near', 0, 0, 0, 1, 3), ('near', 0, 3, 0, 1, 3), ('partner', 0, 0, 1, 0), ('near', 1, 0, 0, 0, 2), ('partner', 0, 0, 1, 3), ('own', 2), ('near', 1, 1, 0, 1, 0), ('near', 2, 0, 0, 0, 2), ('near', 1, 0, 0, 1, 0), ('near', 1, 0, 0, 0, 1), ('near', 2, 1, 0, 0, 2), ('near', 2, 1, 0, 1, 0), ('near', 1, 1, 0, 0, 1), ('partner', 1, 0, 0, 0), ('near', 2, 0, 0, 0, 1), ('near', 2, 1, 0, 0, 1), ('near', 2, 0, 0, 1, 2), ('near', 1, 1, 0, 0, 2), ('near', 2, 1, 0, 1, 2), ('near', 1, 0, 0, 0, 3), ('near', 2, 1, 0, 1, 1), ('near', 2, 0, 0, 1, 1), ('near', 1, 1, 0, 1, 1), ('near', 1, 0, 0, 1, 1), ('near', 1, 1, 0, 0, 3), ('near', 2, 0, 0, 0, 3), ('near', 1, 1, 0, 1, 2), ('partner', 1, 0, 0, 2), ('near', 1, 0, 0, 1, 2), ('partner', 1, 0, 1, 1), ('near', 2, 1, 0, 1, 3), ('near', 1, 1, 0, 1, 3), ('near', 2, 1, 1, 0, 1), ('near', 1, 0, 0, 1, 3), ('partner', 1, 0, 1, 0), ('near', 2, 1, 0, 0, 3), ('near', 2, 0, 1, 0, 0), ('near', 2, 1, 1, 0, 0), ('partner', 1, 0, 0, 1), ('partner', 1, 0, 1, 2), ('near', 2, 0, 1, 1, 1), ('partner', 1, 0, 0, 3), ('near', 2, 0, 0, 1, 3), ('near', 2, 0, 1, 0, 3), ('partner', 1, 0, 1, 3), ('near', 2, 0, 1, 0, 2), ('swap', 1), ('near', 2, 1, 1, 1, 3), ('near', 2, 1, 1, 1, 1), ('near', 2, 1, 1, 0, 3), ('near', 2, 0, 1, 1, 2), ('near', 2, 0, 0, 1, 0), ('near', 2, 0, 1, 0, 1), ('near', 2, 0, 1, 1, 3), ('near', 2, 0, 1, 1, 0), ('near', 2, 1, 1, 1, 0), ('near', 2, 1, 1, 0, 2), ('near', 2, 1, 1, 1, 2), ('partner', 2, 0, 0, 0), ('partner', 2, 0, 0, 1), ('partner', 2, 0, 0, 2), ('partner', 2, 0, 0, 3), ('partner', 2, 0, 1, 0), ('partner', 2, 0, 1, 1), ('partner', 2, 0, 1, 2), ('partner', 2, 0, 1, 3), ('partner', 2, 1, 0, 0), ('partner', 2, 1, 0, 1), ('partner', 2, 1, 0, 2), ('partner', 2, 1, 0, 3), ('partner', 2, 1, 1, 0), ('partner', 2, 1, 1, 1), ('partner', 2, 1, 1, 2), ('partner', 2, 1, 1, 3)]}
 
 
 def schedule(outer):
@@ -110,7 +110,6 @@
     ]
     own[0].start()
     own[1].start()
-    loads[0].start()
 
     x_peer = (1 - rep, me)
     y_peer = (rep, z * 4 + (1 - y) * 2 + c)
@@ -191,6 +190,16 @@
         send(view(kind, block), c_peer, landing(kind, block, 0))
 
     begun = [False, False]
+    waiting = [[], []]
+
+    def catch_up(kind, count):
+        if waiting[kind] and not begun[kind]:
+            loads[kind].wait()
+            if kind == 0:
+                loads[1].start()
+        for block in waiting[kind][:count]:
+            add(kind, block)
+        del waiting[kind][:count]
 
     def add(kind, block):
         value = held[kind, block]
@@ -219,10 +228,15 @@
         send_sem=own_sem.at[2], recv_sem=x_recv,
         device_id=x_peer, device_id_type=MESH,
     )
-    for step in order:
+    for place, step in enumerate(order):
         what, kind = step[0], step[1]
+        if place > HOLD:
+            catch_up(0, 2)
+        if place > HOLD and not waiting[0]:
+            catch_up(1, 1)
         if what == "own":
             if kind == 2:
+                catch_up(0, len(waiting[0]))
                 pre[mine] = acc_a[...].astype(jnp.bfloat16)
             else:
                 own[kind].wait()
@@ -230,10 +244,9 @@
                 forward(kind, unit, 0, 0, 0)
             to_partner(kind, 0, 0, 0)
             if kind < 2:
-                loads[kind].wait()
-                if kind == 0:
-                    loads[1].start()
-                add(kind, me)
+                waiting[kind].append(me)
+            if kind == 0:
+                loads[0].start()
         elif what == "near":
             _, _, unit, r, yy, j = step
             block = block_of(kind, r, yy, j)
@@ -243,14 +256,15 @@
             if arrived[kind, r, yy, j] == PIECES[kind]:
                 to_partner(kind, r, yy, j)
                 if kind < 2:
-                    add(kind, block)
+                    waiting[kind].append(block)
         elif what == "partner":
             _, _, r, yy, j = step
             block = block_of(kind, r, yy, j, True)
             wait(view(kind, block), landing(kind, block, 0))
             if kind < 2:
-                add(kind, block)
-        else:
+                waiting[kind].append(block)
+        else:
+            catch_up(1, len(waiting[1]))
             grad_pre[rep] = acc_g[...].astype(jnp.bfloat16)
             swap.start()
     swap.wait()
@@ -322,7 +336,7 @@
         compiler_params=pltpu.CompilerParams(
             collective_id=0, has_side_effects=True, vmem_limit_bytes=KERNEL_VMEM
         ),
-    )(acts, grads_out, act_inverse, grad_inverse)
+    )(*(pltpu.with_memory_space_constraint(a, pltpu.HBM) for a in (acts, grads_out, act_inverse, grad_inverse)))
     return pl.pallas_call(
         product_kernel,
         out_shape=jax.ShapeDtypeStruct((rows, cols), jnp.float32),

time: 60.1 us -> 57.3 us (0.953)
  local copies, waits for them, and re-layouts: 1.81 us -> 0 us
  Pallas kernels: 58.1 us -> 57.2 us
    unnamed x4 -> x0, local copies, waits for them, and re-layouts: 1.81 us -> none
    pallas_call x1, Pallas kernels: 51.9 us -> 51 us  [fused(): pl.pallas_call(functools.partial(gather_kernel, outer, order), out_shape=...]
where the time goes in v2:
time: 57.3 us; the launch traced here: 57.2 us
  Pallas kernels  57.2 us (100%)
    pallas_call x1, Pallas kernels, fused(): pl.pallas_call(functools.partial(gather_kernel, outer, order), out_shape=...  51 us
    pallas_call x1, Pallas kernels, fused(): pl.pallas_call(product_kernel, out_shape=jax.ShapeDtypeStruct((rows, cols...  6.17 us

profile of v2, /device:TPU:0, one launch (start us, length us, event | category | flops | bytes accessed | tf_op | source)
XLA Modules:
  0.0 57.2 jit_solution(14766466688618187645)
XLA Ops:
  0.0 51.0 %shard_map.46 = (bf16[32,128,512]{2,1,0:T(8,128)(2,1)S(1)}, bf16[2,512,128]{2,1,0:T(8,128)(2,1)S(1)}) custom-call(bf16[128,512]{1,0:T(8,128)(2,1)} %acts.1, bf16[128,512]{1,0:T(8,128)(2,1)} %grads.1, bf16[512,8192]{1,0:T(8,128)(2,1)} %a_hbm.1, bf16[512,8192]{1,0:T(8,128)(2,1)} %g_hbm.1), custom_call_target="tpu_custom_call" | custom-call | tf_op jit(solution)/shard_map/pallas_call | solution.py:315
  51.0 6.2 %shard_map.47 = f32[512,8192]{1,0:T(8,128)} custom-call(bf16[2,512,128]{2,1,0:T(8,128)(2,1)S(1)} %get-tuple-element.7.grad_ref, bf16[2,16,128,512]{3,2,1,0:T(8,128)(2,1)S(1)} %bitcast.1), custom_call_target="tpu_custom_call" | custom-call | tf_op jit(solution)/shard_map/pallas_call | solution.py:340

commit v3 on v2

--- a/solution.py
+++ b/solution.py
@@ -37,9 +37,10 @@
 SWAPPED = (0, 0, 1)
 ROUND_Y, ROUND_Z = 2, 1
 HOLD = 8
+PARTS = (2, 1, 1)
 KERNEL_VMEM = 46137344
 
-ORDERS = {4: [('own', 0), ('near', 0, 0, 0, 0, 1), ('near', 0, 0, 0, 0, 2), ('near', 0, 0, 0, 1, 0), ('near', 0, 1, 0, 0, 2), ('near', 0, 1, 0, 1, 0), ('near', 0, 3, 0, 0, 1), ('near', 0, 1, 0, 0, 1), ('near', 0, 0, 0, 1, 1), ('near', 0, 3, 0, 1, 0), ('near', 0, 2, 0, 0, 2), ('near', 0, 3, 0, 0, 2), ('near', 0, 2, 0, 0, 1), ('partner', 0, 0, 0, 0), ('near', 0, 0, 0, 0, 3), ('near', 0, 1, 0, 0, 3), ('near', 0, 2, 0, 0, 3), ('near', 0, 3, 0, 0, 3), ('near', 0, 1, 0, 1, 2), ('near', 0, 1, 0, 1, 1), ('near', 0, 2, 0, 1, 0), ('near', 0, 3, 0, 1, 2), ('partner', 0, 0, 0, 2), ('near', 0, 3, 0, 1, 1), ('near', 0, 2, 0, 1, 2), ('near', 0, 0, 0, 1, 2), ('own', 1), ('near', 0, 2, 0, 1, 1), ('partner', 0, 0, 0, 1), ('partner', 0, 0, 0, 3), ('partner', 0, 0, 1, 2), ('near', 0, 1, 0, 1, 3), ('partner', 0, 0, 1, 1), ('near', 0, 2, 0, 1, 3), ('near', 0, 0, 0, 1, 3), ('near', 0, 3, 0, 1, 3), ('partner', 0, 0, 1, 0), ('near', 1, 0, 0, 0, 2), ('partner', 0, 0, 1, 3), ('own', 2), ('near', 1, 1, 0, 1, 0), ('near', 2, 0, 0, 0, 2), ('near', 1, 0, 0, 1, 0), ('near', 1, 0, 0, 0, 1), ('near', 2, 1, 0, 0, 2), ('near', 2, 1, 0, 1, 0), ('near', 1, 1, 0, 0, 1), ('partner', 1, 0, 0, 0), ('near', 2, 0, 0, 0, 1), ('near', 2, 1, 0, 0, 1), ('near', 2, 0, 0, 1, 2), ('near', 1, 1, 0, 0, 2), ('near', 2, 1, 0, 1, 2), ('near', 1, 0, 0, 0, 3), ('near', 2, 1, 0, 1, 1), ('near', 2, 0, 0, 1, 1), ('near', 1, 1, 0, 1, 1), ('near', 1, 0, 0, 1, 1), ('near', 1, 1, 0, 0, 3), ('near', 2, 0, 0, 0, 3), ('near', 1, 1, 0, 1, 2), ('partner', 1, 0, 0, 2), ('near', 1, 0, 0, 1, 2), ('partner', 1, 0, 1, 1), ('near', 2, 1, 0, 1, 3), ('near', 1, 1, 0, 1, 3), ('near', 2, 1, 1, 0, 1), ('near', 1, 0, 0, 1, 3), ('partner', 1, 0, 1, 0), ('near', 2, 1, 0, 0, 3), ('near', 2, 0, 1, 0, 0), ('near', 2, 1, 1, 0, 0), ('partner', 1, 0, 0, 1), ('partner', 1, 0, 1, 2), ('near', 2, 0, 1, 1, 1), ('partner', 1, 0, 0, 3), ('near', 2, 0, 0, 1, 3), ('near', 2, 0, 1, 0, 3), ('partner', 1, 0, 1, 3), ('near', 2, 0, 1, 0, 2), ('swap', 1), ('near', 2, 1, 1, 1, 3), ('near', 2, 1, 1, 1, 1), ('near', 2, 1, 1, 0, 3), ('near', 2, 0, 1, 1, 2), ('near', 2, 0, 0, 1, 0), ('near', 2, 0, 1, 0, 1), ('near', 2, 0, 1, 1, 3), ('near', 2, 0, 1, 1, 0), ('near', 2, 1, 1, 1, 0), ('near', 2, 1, 1, 0, 2), ('near', 2, 1, 1, 1, 2), ('partner', 2, 0, 0, 0), ('partner', 2, 0, 0, 1), ('partner', 2, 0, 0, 2), ('partner', 2, 0, 0, 3), ('partner', 2, 0, 1, 0), ('partner', 2, 0, 1, 1), ('partner', 2, 0, 1, 2), ('partner', 2, 0, 1, 3), ('partner', 2, 1, 0, 0), ('partner', 2, 1, 0, 1), ('partner', 2, 1, 0, 2), ('partner', 2, 1, 0, 3), ('partner', 2, 1, 1, 0), ('partner', 2, 1, 1, 1), ('partner', 2, 1, 1, 2), ('partner', 2, 1, 1, 3)]}
+ORDERS = {4: [('own', 0), ('near', 0, 0, 0, 0, 1), ('near', 0, 1, 0, 0, 1), ('near', 0, 1, 0, 1, 0), ('near', 0, 0, 0, 1, 0), ('near', 0, 2, 0, 0, 1), ('near', 0, 1, 0, 0, 2), ('near', 0, 0, 0, 0, 2), ('near', 0, 3, 0, 0, 1), ('near', 0, 0, 0, 1, 1), ('near', 0, 0, 0, 0, 3), ('near', 0, 1, 0, 0, 3), ('partner', 0, 0, 0, 0, 1), ('near', 0, 1, 0, 1, 1), ('near', 0, 3, 0, 0, 2), ('partner', 0, 0, 0, 1, 0), ('near', 0, 1, 0, 1, 2), ('near', 0, 3, 0, 1, 0), ('near', 0, 2, 0, 0, 2), ('near', 0, 2, 0, 0, 3), ('partner', 0, 1, 0, 0, 1), ('partner', 0, 0, 0, 0, 2), ('near', 0, 3, 0, 0, 3), ('own', 1), ('near', 0, 2, 0, 1, 0), ('near', 0, 2, 0, 1, 1), ('near', 0, 3, 0, 1, 1), ('partner', 0, 1, 0, 0, 0), ('partner', 0, 0, 0, 1, 1), ('near', 0, 0, 0, 1, 3), ('partner', 0, 0, 0, 0, 3), ('near', 0, 0, 0, 1, 2), ('partner', 0, 0, 0, 0, 0), ('near', 0, 1, 0, 1, 3), ('partner', 0, 1, 0, 0, 3), ('partner', 0, 0, 0, 1, 2), ('partner', 0, 1, 0, 0, 2), ('partner', 0, 0, 0, 1, 3), ('near', 0, 3, 0, 1, 2), ('partner', 0, 1, 0, 1, 0), ('own', 2, 0), ('near', 0, 2, 0, 1, 2), ('partner', 0, 1, 0, 1, 1), ('near', 0, 3, 0, 1, 3), ('near', 0, 2, 0, 1, 3), ('partner', 0, 1, 0, 1, 2), ('near', 1, 1, 0, 0, 2), ('partner', 0, 1, 0, 1, 3), ('own', 2, 1), ('near', 2, 0, 0, 0, 2), ('near', 1, 0, 0, 1, 0), ('near', 1, 1, 0, 0, 1), ('near', 2, 1, 0, 0, 2), ('near', 2, 0, 0, 0, 1), ('near', 1, 1, 0, 0, 3), ('near', 2, 1, 0, 1, 0), ('near', 2, 1, 0, 0, 1), ('near', 2, 0, 0, 1, 2), ('near', 1, 1, 0, 1, 0), ('near', 1, 0, 0, 0, 1), ('near', 2, 0, 0, 0, 3), ('near', 2, 1, 0, 1, 2), ('near', 2, 0, 0, 1, 1), ('near', 1, 0, 0, 0, 2), ('near', 2, 1, 0, 1, 1), ('partner', 1, 0, 0, 0, 1), ('near', 1, 1, 0, 1, 2), ('near', 1, 0, 0, 0, 3), ('near', 1, 0, 0, 1, 1), ('near', 2, 0, 1, 1, 2), ('partner', 1, 0, 0, 0, 0), ('partner', 1, 0, 0, 0, 2), ('partner', 1, 0, 0, 1, 0), ('near', 2, 1, 0, 0, 3), ('near', 1, 1, 0, 1, 3), ('near', 1, 1, 0, 1, 1), ('near', 2, 1, 0, 1, 3), ('near', 1, 0, 0, 1, 2), ('near', 2, 0, 1, 0, 0), ('near', 2, 0, 1, 1, 1), ('near', 1, 0, 0, 1, 3), ('near', 2, 1, 1, 1, 1), ('near', 2, 1, 1, 0, 0), ('near', 2, 1, 1, 0, 2), ('near', 2, 1, 1, 1, 2), ('near', 2, 0, 0, 1, 3), ('partner', 1, 0, 0, 1, 1), ('partner', 1, 0, 0, 1, 2), ('partner', 1, 0, 0, 0, 3), ('partner', 1, 0, 0, 1, 3), ('swap', 1), ('near', 2, 1, 1, 0, 3), ('near', 2, 1, 1, 1, 3), ('near', 2, 0, 1, 0, 2), ('near', 2, 0, 1, 1, 0), ('near', 2, 0, 1, 0, 3), ('near', 2, 0, 0, 1, 0), ('near', 2, 0, 1, 1, 3), ('near', 2, 0, 1, 0, 1), ('near', 2, 1, 1, 1, 0), ('near', 2, 1, 1, 0, 1), ('partner', 2, 0, 0, 0, 0), ('partner', 2, 0, 0, 0, 1), ('partner', 2, 0, 0, 0, 2), ('partner', 2, 0, 0, 0, 3), ('partner', 2, 0, 0, 1, 0), ('partner', 2, 0, 0, 1, 1), ('partner', 2, 0, 0, 1, 2), ('partner', 2, 0, 0, 1, 3), ('partner', 2, 0, 1, 0, 0), ('partner', 2, 0, 1, 0, 1), ('partner', 2, 0, 1, 0, 2), ('partner', 2, 0, 1, 0, 3), ('partner', 2, 0, 1, 1, 0), ('partner', 2, 0, 1, 1, 1), ('partner', 2, 0, 1, 1, 2), ('partner', 2, 0, 1, 1, 3)]}
 
 
 def schedule(outer):
@@ -77,15 +78,27 @@
     return ways
 
 
+def part_of(kind, unit):
+    return unit * PARTS[kind] // PIECES[kind]
+
+
+def units_of(kind, part=None):
+    if part is None:
+        return range(PIECES[kind])
+    return range(part * PIECES[kind] // PARTS[0], (part + 1) * PIECES[kind] // PARTS[0])
+
+
 def sends_of(order):
     count, seen = 0, {}
     for what, kind, *rest in order:
         if what == "own":
-            count += 1 + sum(len(hops(kind, unit, 0, 0, 0)) for unit in range(PIECES[kind]))
+            units = units_of(kind, *rest)
+            count += sum(len(hops(kind, unit, 0, 0, 0)) for unit in units)
+            count += PARTS[kind] if kind == 0 else PIECES[kind] - 1 in units
         elif what == "near":
-            key = (kind, *rest[1:])
+            key = (kind, part_of(kind, rest[0]), *rest[1:])
             seen[key] = seen.get(key, 0) + 1
-            count += len(hops(kind, *rest)) + (seen[key] == PIECES[kind])
+            count += len(hops(kind, *rest)) + (seen[key] == PIECES[kind] // PARTS[kind])
     return count
 
 
@@ -151,6 +164,12 @@
             return ref
         rows = group // PIECES[kind]
         return ref.at[pl.ds(unit * rows, rows)]
+
+    def part_view(kind, block, part):
+        if PARTS[kind] == 1:
+            return view(kind, block)
+        rows = group // PARTS[kind]
+        return held.at[kind, block, pl.ds(part * rows, rows)]
 
     def landing(kind, block, unit):
         return recv_pre.at[block, unit] if kind == 2 else recv.at[kind, block, unit]
@@ -185,38 +204,42 @@
             peer, when = ways[way]
             send(ref, peer, arrival, when)
 
-    def to_partner(kind, r, yy, j):
+    def to_partner(kind, part, r, yy, j):
         block = block_of(kind, r, yy, j)
-        send(view(kind, block), c_peer, landing(kind, block, 0))
-
-    begun = [False, False]
-    waiting = [[], []]
-
-    def catch_up(kind, count):
-        if waiting[kind] and not begun[kind]:
+        send(part_view(kind, block, part), c_peer, landing(kind, block, part))
+
+    begun = [False] * 3
+    waiting = [[], [], []]
+
+    def catch_up(lot, count):
+        kind = 1 if lot == PARTS[0] else 0
+        if waiting[lot] and not any(begun[:2] if kind == 0 else begun[2:]):
             loads[kind].wait()
             if kind == 0:
                 loads[1].start()
-        for block in waiting[kind][:count]:
-            add(kind, block)
-        del waiting[kind][:count]
-
-    def add(kind, block):
-        value = held[kind, block]
+        for block in waiting[lot][:count]:
+            add(lot, kind, block)
+        del waiting[lot][:count]
+
+    def add(lot, kind, block):
         columns = pl.ds(pl.multiple_of(block * width, width), width)
         if kind == 0:
-            acc, term = acc_a, lax.dot_general(
-                value, a_rows[:, columns], NT, preferred_element_type=jnp.float32
+            rows = group // PARTS[0]
+            span = pl.ds(lot * rows, rows)
+            acc = acc_a.at[span]
+            term = lax.dot_general(
+                held[0, block, span], a_rows[:, columns], NT, preferred_element_type=jnp.float32
             )
         else:
-            acc, term = acc_g, lax.dot_general(
-                g_rows[:, columns], value, NT, preferred_element_type=jnp.float32
+            acc = acc_g
+            term = lax.dot_general(
+                g_rows[:, columns], held[1, block], NT, preferred_element_type=jnp.float32
             )
-        if begun[kind]:
+        if begun[lot]:
             acc[...] += term
         else:
             acc[...] = term
-            begun[kind] = True
+            begun[lot] = True
 
     def wait(ref, arrival):
         pltpu.make_async_copy(ref, ref, arrival).wait()
@@ -228,43 +251,53 @@
         send_sem=own_sem.at[2], recv_sem=x_recv,
         device_id=x_peer, device_id_type=MESH,
     )
+    grad_lot = PARTS[0]
     for place, step in enumerate(order):
         what, kind = step[0], step[1]
         if place > HOLD:
-            catch_up(0, 2)
-        if place > HOLD and not waiting[0]:
-            catch_up(1, 1)
+            lot = next((q for q in range(grad_lot + 1) if waiting[q]), grad_lot)
+            catch_up(lot, 2 if lot < grad_lot else 1)
         if what == "own":
             if kind == 2:
-                catch_up(0, len(waiting[0]))
-                pre[mine] = acc_a[...].astype(jnp.bfloat16)
+                part = step[2]
+                catch_up(part, len(waiting[part]))
+                rows = group // PARTS[0]
+                span = pl.ds(part * rows, rows)
+                pre[mine, span] = acc_a[span].astype(jnp.bfloat16)
             else:
                 own[kind].wait()
-            for unit in range(PIECES[kind]):
+            units = units_of(*step[1:])
+            for unit in units:
                 forward(kind, unit, 0, 0, 0)
-            to_partner(kind, 0, 0, 0)
-            if kind < 2:
-                waiting[kind].append(me)
+            if kind < 2 or PIECES[kind] - 1 in units:
+                for part in range(PARTS[kind]):
+                    to_partner(kind, part, 0, 0, 0)
             if kind == 0:
                 loads[0].start()
+                for part in range(PARTS[0]):
+                    waiting[part].append(me)
+            elif kind == 1:
+                waiting[grad_lot].append(me)
         elif what == "near":
             _, _, unit, r, yy, j = step
             block = block_of(kind, r, yy, j)
             wait(view(kind, block, unit), landing(kind, block, unit))
             forward(kind, unit, r, yy, j)
-            arrived[kind, r, yy, j] = arrived.get((kind, r, yy, j), 0) + 1
-            if arrived[kind, r, yy, j] == PIECES[kind]:
-                to_partner(kind, r, yy, j)
+            part = part_of(kind, unit)
+            key = (kind, part, r, yy, j)
+            arrived[key] = arrived.get(key, 0) + 1
+            if arrived[key] == PIECES[kind] // PARTS[kind]:
+                to_partner(kind, part, r, yy, j)
                 if kind < 2:
-                    waiting[kind].append(block)
+                    waiting[part if kind == 0 else grad_lot].append(block)
         elif what == "partner":
-            _, _, r, yy, j = step
+            _, _, part, r, yy, j = step
             block = block_of(kind, r, yy, j, True)
-            wait(view(kind, block), landing(kind, block, 0))
+            wait(part_view(kind, block, part), landing(kind, block, part))
             if kind < 2:
-                waiting[kind].append(block)
-        else:
-            catch_up(1, len(waiting[1]))
+                waiting[part if kind == 0 else grad_lot].append(block)
+        else:
+            catch_up(grad_lot, len(waiting[grad_lot]))
             grad_pre[rep] = acc_g[...].astype(jnp.bfloat16)
             swap.start()
     swap.wait()

time: 57.3 us -> 55.6 us (0.970)
  Pallas kernels: 57.2 us -> 55.4 us
    pallas_call x1, Pallas kernels: 51 us -> 49.3 us  [fused(): pl.pallas_call(functools.partial(gather_kernel, outer, order), out_shape=...]
where the time goes in v3:
time: 55.6 us; the launch traced here: 55.4 us
  Pallas kernels  55.4 us (100%)
    pallas_call x1, Pallas kernels, fused(): pl.pallas_call(functools.partial(gather_kernel, outer, order), out_shape=...  49.3 us
    pallas_call x1, Pallas kernels, fused(): pl.pallas_call(product_kernel, out_shape=jax.ShapeDtypeStruct((rows, cols...  6.17 us

profile of v3, /device:TPU:0, one launch (start us, length us, event | category | flops | bytes accessed | tf_op | source)
XLA Modules:
  0.0 55.4 jit_solution(14412130814108149108)
XLA Ops:
  0.0 49.3 %shard_map.46 = (bf16[32,128,512]{2,1,0:T(8,128)(2,1)S(1)}, bf16[2,512,128]{2,1,0:T(8,128)(2,1)S(1)}) custom-call(bf16[128,512]{1,0:T(8,128)(2,1)} %acts.1, bf16[128,512]{1,0:T(8,128)(2,1)} %grads.1, bf16[512,8192]{1,0:T(8,128)(2,1)} %a_hbm.1, bf16[512,8192]{1,0:T(8,128)(2,1)} %g_hbm.1), custom_call_target="tpu_custom_call" | custom-call | tf_op jit(solution)/shard_map/pallas_call | solution.py:348
  49.3 6.2 %shard_map.47 = f32[512,8192]{1,0:T(8,128)} custom-call(bf16[2,512,128]{2,1,0:T(8,128)(2,1)S(1)} %get-tuple-element.7.grad_ref, bf16[2,16,128,512]{3,2,1,0:T(8,128)(2,1)S(1)} %bitcast.1), custom_call_target="tpu_custom_call" | custom-call | tf_op jit(solution)/shard_map/pallas_call | solution.py:373

commit v4 on v3

--- a/solution.py
+++ b/solution.py
@@ -37,7 +37,7 @@
 SWAPPED = (0, 0, 1)
 ROUND_Y, ROUND_Z = 2, 1
 HOLD = 8
-PARTS = (2, 1, 1)
+PARTS = (2, 1, 2)
 KERNEL_VMEM = 46137344
 
 ORDERS = {4: [('own', 0), ('near', 0, 0, 0, 0, 1), ('near', 0, 1, 0, 0, 1), ('near', 0, 1, 0, 1, 0), ('near', 0, 0, 0, 1, 0), ('near', 0, 2, 0, 0, 1), ('near', 0, 1, 0, 0, 2), ('near', 0, 0, 0, 0, 2), ('near', 0, 3, 0, 0, 1), ('near', 0, 0, 0, 1, 1), ('near', 0, 0, 0, 0, 3), ('near', 0, 1, 0, 0, 3), ('partner', 0, 0, 0, 0, 1), ('near', 0, 1, 0, 1, 1), ('near', 0, 3, 0, 0, 2), ('partner', 0, 0, 0, 1, 0), ('near', 0, 1, 0, 1, 2), ('near', 0, 3, 0, 1, 0), ('near', 0, 2, 0, 0, 2), ('near', 0, 2, 0, 0, 3), ('partner', 0, 1, 0, 0, 1), ('partner', 0, 0, 0, 0, 2), ('near', 0, 3, 0, 0, 3), ('own', 1), ('near', 0, 2, 0, 1, 0), ('near', 0, 2, 0, 1, 1), ('near', 0, 3, 0, 1, 1), ('partner', 0, 1, 0, 0, 0), ('partner', 0, 0, 0, 1, 1), ('near', 0, 0, 0, 1, 3), ('partner', 0, 0, 0, 0, 3), ('near', 0, 0, 0, 1, 2), ('partner', 0, 0, 0, 0, 0), ('near', 0, 1, 0, 1, 3), ('partner', 0, 1, 0, 0, 3), ('partner', 0, 0, 0, 1, 2), ('partner', 0, 1, 0, 0, 2), ('partner', 0, 0, 0, 1, 3), ('near', 0, 3, 0, 1, 2), ('partner', 0, 1, 0, 1, 0), ('own', 2, 0), ('near', 0, 2, 0, 1, 2), ('partner', 0, 1, 0, 1, 1), ('near', 0, 3, 0, 1, 3), ('near', 0, 2, 0, 1, 3), ('partner', 0, 1, 0, 1, 2), ('near', 1, 1, 0, 0, 2), ('partner', 0, 1, 0, 1, 3), ('own', 2, 1), ('near', 2, 0, 0, 0, 2), ('near', 1, 0, 0, 1, 0), ('near', 1, 1, 0, 0, 1), ('near', 2, 1, 0, 0, 2), ('near', 2, 0, 0, 0, 1), ('near', 1, 1, 0, 0, 3), ('near', 2, 1, 0, 1, 0), ('near', 2, 1, 0, 0, 1), ('near', 2, 0, 0, 1, 2), ('near', 1, 1, 0, 1, 0), ('near', 1, 0, 0, 0, 1), ('near', 2, 0, 0, 0, 3), ('near', 2, 1, 0, 1, 2), ('near', 2, 0, 0, 1, 1), ('near', 1, 0, 0, 0, 2), ('near', 2, 1, 0, 1, 1), ('partner', 1, 0, 0, 0, 1), ('near', 1, 1, 0, 1, 2), ('near', 1, 0, 0, 0, 3), ('near', 1, 0, 0, 1, 1), ('near', 2, 0, 1, 1, 2), ('partner', 1, 0, 0, 0, 0), ('partner', 1, 0, 0, 0, 2), ('partner', 1, 0, 0, 1, 0), ('near', 2, 1, 0, 0, 3), ('near', 1, 1, 0, 1, 3), ('near', 1, 1, 0, 1, 1), ('near', 2, 1, 0, 1, 3), ('near', 1, 0, 0, 1, 2), ('near', 2, 0, 1, 0, 0), ('near', 2, 0, 1, 1, 1), ('near', 1, 0, 0, 1, 3), ('near', 2, 1, 1, 1, 1), ('near', 2, 1, 1, 0, 0), ('near', 2, 1, 1, 0, 2), ('near', 2, 1, 1, 1, 2), ('near', 2, 0, 0, 1, 3), ('partner', 1, 0, 0, 1, 1), ('partner', 1, 0, 0, 1, 2), ('partner', 1, 0, 0, 0, 3), ('partner', 1, 0, 0, 1, 3), ('swap', 1), ('near', 2, 1, 1, 0, 3), ('near', 2, 1, 1, 1, 3), ('near', 2, 0, 1, 0, 2), ('near', 2, 0, 1, 1, 0), ('near', 2, 0, 1, 0, 3), ('near', 2, 0, 0, 1, 0), ('near', 2, 0, 1, 1, 3), ('near', 2, 0, 1, 0, 1), ('near', 2, 1, 1, 1, 0), ('near', 2, 1, 1, 0, 1), ('partner', 2, 0, 0, 0, 0), ('partner', 2, 0, 0, 0, 1), ('partner', 2, 0, 0, 0, 2), ('partner', 2, 0, 0, 0, 3), ('partner', 2, 0, 0, 1, 0), ('partner', 2, 0, 0, 1, 1), ('partner', 2, 0, 0, 1, 2), ('partner', 2, 0, 0, 1, 3), ('partner', 2, 0, 1, 0, 0), ('partner', 2, 0, 1, 0, 1), ('partner', 2, 0, 1, 0, 2), ('partner', 2, 0, 1, 0, 3), ('partner', 2, 0, 1, 1, 0), ('partner', 2, 0, 1, 1, 1), ('partner', 2, 0, 1, 1, 2), ('partner', 2, 0, 1, 1, 3)]}
@@ -94,7 +94,7 @@
         if what == "own":
             units = units_of(kind, *rest)
             count += sum(len(hops(kind, unit, 0, 0, 0)) for unit in units)
-            count += PARTS[kind] if kind == 0 else PIECES[kind] - 1 in units
+            count += len(rest) or PARTS[kind]
         elif what == "near":
             key = (kind, part_of(kind, rest[0]), *rest[1:])
             seen[key] = seen.get(key, 0) + 1
@@ -169,7 +169,7 @@
         if PARTS[kind] == 1:
             return view(kind, block)
         rows = group // PARTS[kind]
-        return held.at[kind, block, pl.ds(part * rows, rows)]
+        return view(kind, block).at[pl.ds(part * rows, rows)]
 
     def landing(kind, block, unit):
         return recv_pre.at[block, unit] if kind == 2 else recv.at[kind, block, unit]
@@ -269,9 +269,8 @@
             units = units_of(*step[1:])
             for unit in units:
                 forward(kind, unit, 0, 0, 0)
-            if kind < 2 or PIECES[kind] - 1 in units:
-                for part in range(PARTS[kind]):
-                    to_partner(kind, part, 0, 0, 0)
+            for part in step[2:] or range(PARTS[kind]):
+                to_partner(kind, part, 0, 0, 0)
             if kind == 0:
                 loads[0].start()
                 for part in range(PARTS[0]):
@@ -293,7 +292,8 @@
         elif what == "partner":
             _, _, part, r, yy, j = step
             block = block_of(kind, r, yy, j, True)
-            wait(part_view(kind, block, part), landing(kind, block, part))
+            for half in range(PARTS[2]) if kind == 2 else [part]:
+                wait(part_view(kind, block, half), landing(kind, block, half))
             if kind < 2:
                 waiting[part if kind == 0 else grad_lot].append(block)
         else:

time: 55.6 us -> 55.8 us (level)
  no operation moved by 1% of the time
where the time goes in v4:
time: 55.8 us; the launch traced here: 55.7 us
  Pallas kernels  55.7 us (100%)
    pallas_call x1, Pallas kernels, fused(): pl.pallas_call(functools.partial(gather_kernel, outer, order), out_shape=...  49.5 us
    pallas_call x1, Pallas kernels, fused(): pl.pallas_call(product_kernel, out_shape=jax.ShapeDtypeStruct((rows, cols...  6.17 us

profile of v4, /device:TPU:0, one launch (start us, length us, event | category | flops | bytes accessed | tf_op | source)
XLA Modules:
  0.0 55.7 jit_solution(3578312726072427226)
XLA Ops:
  0.0 49.5 %shard_map.46 = (bf16[32,128,512]{2,1,0:T(8,128)(2,1)S(1)}, bf16[2,512,128]{2,1,0:T(8,128)(2,1)S(1)}) custom-call(bf16[128,512]{1,0:T(8,128)(2,1)} %acts.1, bf16[128,512]{1,0:T(8,128)(2,1)} %grads.1, bf16[512,8192]{1,0:T(8,128)(2,1)} %a_hbm.1, bf16[512,8192]{1,0:T(8,128)(2,1)} %g_hbm.1), custom_call_target="tpu_custom_call" | custom-call | tf_op jit(solution)/shard_map/pallas_call | solution.py:348
  49.5 6.2 %shard_map.47 = f32[512,8192]{1,0:T(8,128)} custom-call(bf16[2,512,128]{2,1,0:T(8,128)(2,1)S(1)} %get-tuple-element.7.grad_ref, bf16[2,16,128,512]{3,2,1,0:T(8,128)(2,1)S(1)} %bitcast.1), custom_call_target="tpu_custom_call" | custom-call | tf_op jit(solution)/shard_map/pallas_call | solution.py:373

commit v5 on v3

--- a/solution.py
+++ b/solution.py
@@ -308,7 +308,7 @@
             pl.when(when)(copy.wait_send)
 
 
-SLOTS = 4
+SLOTS = 8
 
 
 def product_kernel(grad_ref, act_ref, out_hbm, tiles, sems):

time: 55.6 us -> 55.6 us (level)
  no operation moved by 1% of the time
where the time goes in v5:
time: 55.6 us; the launch traced here: 55.5 us
  Pallas kernels  55.5 us (100%)
    pallas_call x1, Pallas kernels, fused(): pl.pallas_call(functools.partial(gather_kernel, outer, order), out_shape=...  49.3 us
    pallas_call x1, Pallas kernels, fused(): pl.pallas_call(product_kernel, out_shape=jax.ShapeDtypeStruct((rows, cols...  6.19 us

profile of v5, /device:TPU:0, one launch (start us, length us, event | category | flops | bytes accessed | tf_op | source)
XLA Modules:
  0.0 55.5 jit_solution(17905687947999751212)
XLA Ops:
  0.0 49.3 %shard_map.46 = (bf16[32,128,512]{2,1,0:T(8,128)(2,1)S(1)}, bf16[2,512,128]{2,1,0:T(8,128)(2,1)S(1)}) custom-call(bf16[128,512]{1,0:T(8,128)(2,1)} %acts.1, bf16[128,512]{1,0:T(8,128)(2,1)} %grads.1, bf16[512,8192]{1,0:T(8,128)(2,1)} %a_hbm.1, bf16[512,8192]{1,0:T(8,128)(2,1)} %g_hbm.1), custom_call_target="tpu_custom_call" | custom-call | tf_op jit(solution)/shard_map/pallas_call | solution.py:348
  49.3 6.2 %shard_map.47 = f32[512,8192]{1,0:T(8,128)} custom-call(bf16[2,512,128]{2,1,0:T(8,128)(2,1)S(1)} %get-tuple-element.7.grad_ref, bf16[2,16,128,512]{3,2,1,0:T(8,128)(2,1)S(1)} %bitcast.1), custom_call_target="tpu_custom_call" | custom-call | tf_op jit(solution)/shard_map/pallas_call | solution.py:373
